TPU v7x, 32 devices: a whole 2x2x4 slice. The times are simulated.
32 devices in a mesh: data: 2 (over x), seq: 4 (over z), branch: 4 (over y, core).
Axes of the slice: x: 2, y: 2, z: 4, core: 2. Of those that a mesh axis runs over, the one named last changes fastest.
Arguments:
- latents: bfloat16 [2, 1024, 2432], P('data', ('seq', 'branch')), parts along dimension 0
- hint_emb: bfloat16 [2, 1024, 2432], P('data', ('seq', 'branch')), parts along dimension 0
- in_qkv: bfloat16 [2, 3, 2432, 7296], replicated
- in_proj: bfloat16 [2, 3, 38, 64, 2432], replicated
- in_up: bfloat16 [2, 3, 2432, 9728], replicated
- in_down: bfloat16 [2, 3, 9728, 2432], replicated
- out_qkv: bfloat16 [2, 2432, 7296], replicated
- out_proj: bfloat16 [2, 38, 64, 2432], replicated
- out_up: bfloat16 [2, 2432, 9728], replicated
- out_down: bfloat16 [2, 9728, 2432], replicated
- hint_proj: bfloat16 [2432, 2432], replicated
- zero_proj: bfloat16 [3, 2432, 2432], replicated
- skip_proj: bfloat16 [2, 4864, 2432], replicated
- final_proj: bfloat16 [2432, 2432], replicated
Outputs:
- output: bfloat16 [2, 1024, 2432], P('data', ('seq', 'branch')), parts along dimension 0
There are 2 independent parts. A program takes and returns all parts, laid end to end along the dimension named above; an argument that names none is the same for every part.
All inputs are finite; a program needn't handle non-finite values.
Results may differ from a plain program's by a relative error of at most 0.02.
Values are sent between devices in bfloat16 or wider.
A program may use at most 4.75 GiB of HBM per device.

v0:
```python
import jax
import jax.numpy as jnp
from jax import lax
from jax.sharding import PartitionSpec as P

EPS = 1e-6


def layer_norm(values):
    values = values.astype(jnp.float32)
    mean_val = jnp.mean(values, axis=-1, keepdims=True)
    centered = values - mean_val
    var_val = jnp.mean(centered * centered, axis=-1, keepdims=True)
    return (centered * lax.rsqrt(var_val + EPS)).astype(jnp.bfloat16)


def add_bf16(left_op, right_op):
    return (left_op.astype(jnp.float32) + right_op.astype(jnp.float32)).astype(jnp.bfloat16)


def project(act_rows, weight):
    return jnp.einsum('...d,de->...e', act_rows, weight, preferred_element_type=jnp.float32).astype(jnp.bfloat16)


def run_block(residual, w_qkv, w_proj, w_up, w_down, gather_kv):
    model_width = residual.shape[-1]
    num_heads = w_proj.shape[0]
    head_dim = model_width // num_heads
    row_count = residual.shape[0]
    qkv_rows = project(layer_norm(residual), w_qkv)
    kv_all = gather_kv(qkv_rows[:, model_width:])
    key_count = kv_all.shape[0]
    q_heads = qkv_rows[:, :model_width].reshape(row_count, num_heads, head_dim)
    k_heads = kv_all[:, :model_width].reshape(key_count, num_heads, head_dim)
    v_heads = kv_all[:, model_width:].reshape(key_count, num_heads, head_dim)
    scores = jnp.einsum('qhc,khc->hqk', q_heads, k_heads, preferred_element_type=jnp.float32) * (head_dim ** -0.5)
    attn_probs = jax.nn.softmax(scores, axis=-1).astype(jnp.bfloat16)
    mixed_rows = jnp.einsum('hqk,khc->qhc', attn_probs, v_heads, preferred_element_type=jnp.float32).astype(jnp.bfloat16)
    attn_out = jnp.einsum('qhc,hcd->qd', mixed_rows, w_proj, preferred_element_type=jnp.float32).astype(jnp.bfloat16)
    residual = add_bf16(residual, attn_out)
    activated = jax.nn.gelu(project(layer_norm(residual), w_up).astype(jnp.float32)).astype(jnp.bfloat16)
    return add_bf16(residual, project(activated, w_down))


def solution(mesh):
    group_size = mesh.shape['branch']
    half_size = group_size // 2
    levels = half_size.bit_length() - 1
    swap_perm = [(dev_index, (dev_index + half_size) % group_size) for dev_index in range(group_size)]
    hint_perm = [(dev_index, dev_index + half_size) for dev_index in range(half_size)]
    level_perms = [[(dev_index, dev_index ^ (1 << level_no)) for dev_index in range(group_size)] for level_no in range(levels)]
    row_spec = P('data', ('seq', 'branch'), None)

    def gather_branch(kv_rows):
        gathered = lax.all_gather(kv_rows, 'seq', axis=0, tiled=True)
        for level_perm in level_perms:
            gathered = jnp.concatenate([gathered, lax.ppermute(gathered, 'branch', level_perm)], axis=0)
        return gathered

    def gather_image(kv_rows):
        return lax.all_gather(kv_rows, ('seq', 'branch'), axis=0, tiled=True)

    def device_fn(latents, hint_emb, in_qkv, in_proj, in_up, in_down, out_qkv, out_proj, out_up, out_down, hint_proj, zero_proj, skip_proj, final_proj):
        num_in = out_qkv.shape[0]
        branch_side = lax.axis_index('branch') // half_size
        is_control = branch_side == 1
        own_lat = latents[0]
        own_hint = hint_emb[0]
        own_count = own_lat.shape[0]
        pair_lat = jnp.concatenate([own_lat, lax.ppermute(own_lat, 'branch', swap_perm)], axis=0)
        recv_hint = lax.ppermute(own_hint, 'branch', hint_perm)
        residual = lax.cond(is_control, lambda: add_bf16(pair_lat, project(jnp.concatenate([own_hint, recv_hint], axis=0), hint_proj)), lambda: pair_lat)
        own_parts = []
        for block_no in range(num_in + 1):
            residual = run_block(residual, in_qkv[branch_side, block_no], in_proj[branch_side, block_no], in_up[branch_side, block_no], in_down[branch_side, block_no], gather_branch)
            own_parts.append(lax.cond(is_control, lambda act_rows: project(act_rows, zero_proj[block_no]), lambda act_rows: act_rows, residual))
        part_stack = jnp.stack(own_parts)
        received = lax.ppermute(part_stack[:, own_count:], 'branch', swap_perm)
        skip_sums = add_bf16(part_stack[:, :own_count], received)
        outputs = skip_sums[num_in]
        for out_no in range(num_in):
            merged = project(jnp.concatenate([outputs, skip_sums[num_in - 1 - out_no]], axis=-1), skip_proj[out_no])
            outputs = run_block(merged, out_qkv[out_no], out_proj[out_no], out_up[out_no], out_down[out_no], gather_image)
        return project(layer_norm(outputs), final_proj)[None]

    return jax.shard_map(device_fn, mesh=mesh, in_specs=(row_spec, row_spec) + (P(),) * 12, out_specs=row_spec, check_vma=False)
```

profile of v0, /device:TPU:0, one launch (start us, length us, event | category | flops | bytes accessed | tf_op | source)
XLA Modules:
  0.0 1073.6 jit_solution(8844897110400466313)
XLA Ops:
  23.4 13.9 %fusion.151 = bf16[128,7296]{1,0:T(8,128)(2,1)S(1)} fusion(bf16[2,3,2432,7296]{3,2,1,0:T(8,128)(2,1)} %param.24, s32[]{:T(128)S(6)} %select_n.8, f32[128,2432]{1,0:T(8,128)S(1)} %get-tuple-element.93, f32[128]{0:T(128)S(1)} %add_rsqrt_fusion.10, f32[128]{0:T(128)S(1)} %broadcast_multiply_fusion.10), kind=kOutput, calls=%fused_computation.127 | convolution fusion | flops 4544299008 | bytes 38601732 | tf_op jit(solution)/shard_map/...d,de->...e/dot_general | solution.py:22
  39.1 101.3 %all-gather.6.cloned.1.call-done = bf16[512,4864]{1,0:T(8,128)(2,1)} async-done(((bf16[128,4864]{1,0:T(8,128)(2,1)}), bf16[512,4864]{1,0:T(8,128)(2,1)}) %all-gather.6.cloned.1.call-update) | async-done | bytes 4980752 | tf_op jit(solution)/shard_map/all_gather | solution.py:55
  153.6 8.4 fusion.567
  177.1 11.9 %fusion.568 = (f32[38,128]{1,0:T(8,128)S(1)}, f32[38,128,1024]{2,1,0:T(8,128)}) fusion(bf16[128,38,64]{0,2,1:T(8,128)(2,1)S(1)} %bitcast.467, bf16[1024,38,64]{0,2,1:T(8,128)(2,1)} %bitcast.462), kind=kOutput, calls=%fused_computation.412 | convolution fusion | flops 652477440 | bytes 25545728 | tf_op jit(solution)/shard_map/sub | solution.py:37
  189.1 14.5 %fusion.569 = (f32[128]{0:T(128)S(1)}, f32[128,2432]{1,0:T(8,128)S(1)}) fusion(f32[128,2432]{1,0:T(8,128)S(1)} %get-tuple-element.93, bf16[2,3,38,64,2432]{4,3,2,1,0:T(8,128)(2,1)} %param.25, s32[]{:T(128)S(6)} %select_n.8, bf16[1024,38,64]{0,2,1:T(8,128)(2,1)} %bitcast.459, f32[38,128,1024]{2,1,0:T(8,128)} %get-tuple-element.114, ...), kind=kOutput, calls=%fused_computation.413 | convolution fusion | flops 2163818496 | bytes 39243268 | tf_op jit(solution)/shard_map/qhc,hcd->qd/dot_general | solution.py:39
  203.9 31.4 %convert_reduce_fusion.1 = (f32[128]{0:T(128)S(1)}, bf16[128,2432]{1,0:T(8,128)(2,1)S(1)}) fusion(f32[128,2432]{1,0:T(8,128)S(1)} %get-tuple-element.116, bf16[2,3,9728,2432]{3,2,1,0:T(8,128)(2,1)} %param.27, s32[]{:T(128)S(6)} %select_n.8, bf16[2,3,2432,9728]{3,2,1,0:T(8,128)(2,1)} %param.26, f32[128]{0:T(128)S(1)} %add_rsqrt_fusion.9, ...), kind=kOutput, calls=%fused_computation.261 | convolution fusion | flops 12129648640 | bytes 97749504 | tf_op jit(solution)/shard_map/...d,de->...e/dot_general | solution.py:22
  235.6 14.1 %fusion.154 = bf16[128,7296]{1,0:T(8,128)(2,1)S(1)} fusion(bf16[2,3,2432,7296]{3,2,1,0:T(8,128)(2,1)} %param.24, s32[]{:T(128)S(6)} %select_n.8, bf16[128,2432]{1,0:T(8,128)(2,1)S(1)} %get-tuple-element.118, f32[128]{0:T(128)S(1)} %add_rsqrt_fusion.8, f32[128]{0:T(128)S(1)} %broadcast_multiply_fusion.8), kind=kOutput, calls=%fused_computation.128 | convolution fusion | flops 4544610304 | bytes 37979140 | tf_op jit(solution)/shard_map/...d,de->...e/dot_general | solution.py:22
  251.0 92.1 %all-gather.8.cloned.1.call-done = bf16[512,4864]{1,0:T(8,128)(2,1)} async-done(((bf16[128,4864]{1,0:T(8,128)(2,1)}), bf16[512,4864]{1,0:T(8,128)(2,1)}) %all-gather.8.cloned.1.call-update) | async-done | bytes 4980752 | tf_op jit(solution)/shard_map/all_gather | solution.py:55
  356.3 8.4 fusion.566
  379.8 11.9 %fusion.572 = (f32[38,128]{1,0:T(8,128)S(1)}, f32[38,128,1024]{2,1,0:T(8,128)}) fusion(bf16[128,38,64]{0,2,1:T(8,128)(2,1)S(1)} %bitcast.468, bf16[1024,38,64]{0,2,1:T(8,128)(2,1)} %bitcast.463), kind=kOutput, calls=%fused_computation.414 | convolution fusion | flops 652477440 | bytes 25545728 | tf_op jit(solution)/shard_map/sub | solution.py:37
  391.7 14.5 %fusion.573 = (f32[128]{0:T(128)S(1)}, f32[128,2432]{1,0:T(8,128)S(1)}) fusion(bf16[2,3,38,64,2432]{4,3,2,1,0:T(8,128)(2,1)} %param.25, s32[]{:T(128)S(6)} %select_n.8, bf16[1024,38,64]{0,2,1:T(8,128)(2,1)} %bitcast.460, f32[38,128,1024]{2,1,0:T(8,128)} %get-tuple-element.120, f32[38,128]{1,0:T(8,128)S(1)} %get-tuple-element.119, ...), kind=kOutput, calls=%fused_computation.415 | convolution fusion | flops 2164129792 | bytes 38620676 | tf_op jit(solution)/shard_map/qhc,hcd->qd/dot_general | solution.py:39
  406.5 31.2 %convert_reduce_fusion = (f32[128]{0:T(128)S(1)}, bf16[128,2432]{1,0:T(8,128)(2,1)S(1)}) fusion(f32[128,2432]{1,0:T(8,128)S(1)} %get-tuple-element.122, bf16[2,3,9728,2432]{3,2,1,0:T(8,128)(2,1)} %param.27, s32[]{:T(128)S(6)} %select_n.8, bf16[2,3,2432,9728]{3,2,1,0:T(8,128)(2,1)} %param.26, f32[128]{0:T(128)S(1)} %add_rsqrt_fusion.7, ...), kind=kOutput, calls=%fused_computation.259 | convolution fusion | flops 12129648640 | bytes 97749504 | tf_op jit(solution)/shard_map/...d,de->...e/dot_general | solution.py:22
  438.1 14.2 %fusion.157 = bf16[128,7296]{1,0:T(8,128)(2,1)S(1)} fusion(bf16[2,3,2432,7296]{3,2,1,0:T(8,128)(2,1)} %param.24, s32[]{:T(128)S(6)} %select_n.8, bf16[128,2432]{1,0:T(8,128)(2,1)S(1)} %get-tuple-element.124, f32[128]{0:T(128)S(1)} %add_rsqrt_fusion.6, f32[128]{0:T(128)S(1)} %broadcast_multiply_fusion.6), kind=kOutput, calls=%fused_computation.129 | convolution fusion | flops 4544610304 | bytes 37979140 | tf_op jit(solution)/shard_map/...d,de->...e/dot_general | solution.py:22
  453.6 92.4 %all-gather.10.cloned.1.call-done = bf16[512,4864]{1,0:T(8,128)(2,1)} async-done(((bf16[128,4864]{1,0:T(8,128)(2,1)}), bf16[512,4864]{1,0:T(8,128)(2,1)}) %all-gather.10.cloned.1.call-update) | async-done | bytes 4980752 | tf_op jit(solution)/shard_map/all_gather | solution.py:55
  559.8 8.4 fusion.565
  583.7 12.1 %fusion.576 = (f32[38,128]{1,0:T(8,128)S(1)}, f32[38,128,1024]{2,1,0:T(8,128)}) fusion(bf16[128,38,64]{0,2,1:T(8,128)(2,1)} %bitcast.466, bf16[1024,38,64]{0,2,1:T(8,128)(2,1)} %bitcast.464), kind=kOutput, calls=%fused_computation.416 | convolution fusion | flops 652477440 | bytes 25545728 | tf_op jit(solution)/shard_map/sub | solution.py:37
  595.8 15.6 %fusion.577 = (f32[128]{0:T(128)S(1)}, f32[128,2432]{1,0:T(8,128)}) fusion(bf16[2,3,38,64,2432]{4,3,2,1,0:T(8,128)(2,1)} %param.25, s32[]{:T(128)S(6)} %select_n.8, bf16[1024,38,64]{0,2,1:T(8,128)(2,1)} %bitcast.461, f32[38,128,1024]{2,1,0:T(8,128)} %get-tuple-element.126, f32[38,128]{1,0:T(8,128)S(1)} %get-tuple-element.125, ...), kind=kOutput, calls=%fused_computation.417 | convolution fusion | flops 2164129792 | bytes 38620676 | tf_op jit(solution)/shard_map/qhc,hcd->qd/dot_general | solution.py:39
  613.0 35.7 %fusion.327 = bf16[128,2432]{1,0:T(8,128)(2,1)S(1)} fusion(f32[128,2432]{1,0:T(8,128)} %get-tuple-element.128, bf16[2,3,9728,2432]{3,2,1,0:T(8,128)(2,1)} %param.27, s32[]{:T(128)S(6)} %select_n.8, bf16[2,3,2432,9728]{3,2,1,0:T(8,128)(2,1)} %param.26, f32[128]{0:T(128)S(1)} %add_rsqrt_fusion.5, f32[128]{0:T(128)S(1)} %broadcast_multiply_fusion.5), kind=kOutput, calls=%fused_computation.198 | convolution fusion | flops 12129026048 | bytes 97748992 | tf_op jit(solution)/shard_map/...d,de->...e/dot_general | solution.py:22
  649.1 20.8 %collective-permute-start.5 = (bf16[3,64,2432]{2,1,0:T(8,128)(2,1)S(1)}, bf16[3,64,2432]{2,1,0:T(8,128)(2,1)S(1)}, u32[]{:S(2)}, u32[]{:S(2)}) collective-permute-start(bf16[3,64,2432]{2,1,0:T(8,128)(2,1)S(1)} %slice.162), channel_id=1, source_target_pairs={{0,2},{1,3},{2,0},{3,1},{4,6},{5,7},{6,4},{7,5},{8,10},{9,11},{10,... | collective-permute-start | bytes 2801672 | tf_op jit(solution)/shard_map/ppermute | solution.py:78
  669.9 21.4 %collective-permute-done.5 = bf16[3,64,2432]{2,1,0:T(8,128)(2,1)S(1)} collective-permute-done((bf16[3,64,2432]{2,1,0:T(8,128)(2,1)S(1)}, bf16[3,64,2432]{2,1,0:T(8,128)(2,1)S(1)}, u32[]{:S(2)}, u32[]{:S(2)}) %collective-permute-start.5) | collective-permute-done | bytes 933920 | tf_op jit(solution)/shard_map/ppermute | solution.py:78
  691.6 10.2 fusion.578
  702.1 14.5 %fusion.160 = bf16[64,7296]{1,0:T(8,128)(2,1)S(1)} fusion(bf16[2,2432,7296]{2,1,0:T(8,128)(2,1)} %param.28, f32[64,2432]{1,0:T(8,128)S(1)} %get-tuple-element.130, f32[64]{0:T(128)S(1)} %add_rsqrt_fusion.4, f32[64]{0:T(128)S(1)} %broadcast_multiply_fusion.4), kind=kOutput, calls=%fused_computation.130 | convolution fusion | flops 2272149504 | bytes 37044736 | tf_op jit(solution)/shard_map/...d,de->...e/dot_general | solution.py:22
  718.2 82.3 %all-gather.12.cloned.1.call-done = bf16[1024,4864]{1,0:T(8,128)(2,1)} async-done(((bf16[64,4864]{1,0:T(8,128)(2,1)}), bf16[1024,4864]{1,0:T(8,128)(2,1)}) %all-gather.12.cloned.1.call-update) | async-done | bytes 9961488 | tf_op jit(solution)/shard_map/all_gather | solution.py:61
  800.6 8.3 fusion.564
  832.9 10.7 fusion.580
  843.9 31.8 %fusion.389 = bf16[64,2432]{1,0:T(8,128)(2,1)S(1)} fusion(f32[64,2432]{1,0:T(8,128)S(1)} %get-tuple-element.134, bf16[2,9728,2432]{2,1,0:T(8,128)(2,1)} %param.31, bf16[2,2432,9728]{2,1,0:T(8,128)(2,1)} %param.30, f32[64]{0:T(128)S(1)} %add_rsqrt_fusion.3, f32[64]{0:T(128)S(1)} %broadcast_multiply_fusion.3), kind=kOutput, calls=%fused_computation.218 | convolution fusion | flops 6064513024 | bytes 96191488 | tf_op jit(solution)/shard_map/...d,de->...e/dot_general | solution.py:22
  875.7 10.2 fusion.581
  886.1 14.8 %fusion.163 = bf16[64,7296]{1,0:T(8,128)(2,1)S(1)} fusion(bf16[2,2432,7296]{2,1,0:T(8,128)(2,1)} %param.28, f32[64,2432]{1,0:T(8,128)S(1)} %get-tuple-element.136, f32[64]{0:T(128)S(1)} %add_rsqrt_fusion.2, f32[64]{0:T(128)S(1)} %broadcast_multiply_fusion.2), kind=kOutput, calls=%fused_computation.131 | convolution fusion | flops 2272149504 | bytes 37044736 | tf_op jit(solution)/shard_map/...d,de->...e/dot_general | solution.py:22
  902.3 82.0 %all-gather.14.cloned.1.call-done = bf16[1024,4864]{1,0:T(8,128)(2,1)} async-done(((bf16[64,4864]{1,0:T(8,128)(2,1)}), bf16[1024,4864]{1,0:T(8,128)(2,1)}) %all-gather.14.cloned.1.call-update) | async-done | bytes 9961488 | tf_op jit(solution)/shard_map/all_gather | solution.py:61
  984.3 8.3 fusion.563
  1016.6 10.7 fusion.583
  1027.6 32.0 %fusion.584 = (f32[64]{0:T(128)S(1)}, f32[64,2432]{1,0:T(8,128)S(1)}) fusion(f32[64,2432]{1,0:T(8,128)S(1)} %get-tuple-element.140, bf16[2,9728,2432]{2,1,0:T(8,128)(2,1)} %param.31, bf16[2,2432,9728]{2,1,0:T(8,128)(2,1)} %param.30, f32[64]{0:T(128)S(1)} %add_rsqrt_fusion.1, f32[64]{0:T(128)S(1)} %broadcast_multiply_fusion.1), kind=kOutput, calls=%fused_computation.424 | convolution fusion | flops 6064824320 | bytes 96503040 | tf_op jit(solution)/shard_map/...d,de->...e/dot_general | solution.py:22
  (111 shorter events, 169.9 us)
Async XLA Ops:
  6.5 133.9 %all-gather.6.cloned.1.call-start = ((), (), s32[]{:S(2)}) async-start(), calls=%async_computation | async-start | bytes 6225920 | tf_op jit(solution)/shard_map/all_gather | solution.py:55
  6.5 10.8 %collective-permute-start = (bf16[64,2432]{1,0:T(8,128)(2,1)}, bf16[64,2432]{1,0:T(8,128)(2,1)S(1)}, u32[]{:S(2)}, u32[]{:S(2)}) collective-permute-start(bf16[64,2432]{1,0:T(8,128)(2,1)} %bitcast.471), channel_id=1, source_target_pairs={{0,2},{1,3},{2,0},{3,1},{4,6},{5,7},{6,4},{7,5},{8,10},{9,11},{10,... | collective-permute-start | bytes 933896 | tf_op jit(solution)/shard_map/ppermute | solution.py:70
  9.6 13.3 %collective-permute-start.1 = (bf16[64,2432]{1,0:T(8,128)(2,1)}, bf16[64,2432]{1,0:T(8,128)(2,1)S(1)}, u32[]{:S(2)}, u32[]{:S(2)}) collective-permute-start(bf16[64,2432]{1,0:T(8,128)(2,1)} %bitcast.469), channel_id=1, source_target_pairs={{0,2},{1,3},{4,6},{5,7},{8,10},{9,11},{12,14},{13,15},{16,18},{17,... | collective-permute-start | bytes 933896 | tf_op jit(solution)/shard_map/ppermute | solution.py:71
  37.3 103.1 %copy-start.1 = (bf16[128,7296]{1,0:T(8,128)(2,1)}, bf16[128,7296]{1,0:T(8,128)(2,1)S(1)}, u32[]{:S(2)}) copy-start(bf16[128,7296]{1,0:T(8,128)(2,1)S(1)} %fusion.151) | copy-start | bytes 5603332
  38.6 304.5 %all-gather.8.cloned.1.call-start = ((), (), s32[]{:S(2)}) async-start(), calls=%async_computation.1 | async-start | bytes 6225920 | tf_op jit(solution)/shard_map/all_gather | solution.py:55
  140.4 8.2 collective-permute-start.2
  250.9 295.0 %all-gather.10.cloned.1.call-start = ((), (), s32[]{:S(2)}) async-start(), calls=%async_computation.2 | async-start | bytes 6225920 | tf_op jit(solution)/shard_map/all_gather | solution.py:55
  343.1 8.2 collective-permute-start.3
  452.3 94.5 %copy-start = (bf16[128,7296]{1,0:T(8,128)(2,1)}, bf16[128,7296]{1,0:T(8,128)(2,1)S(1)}, u32[]{:S(2)}) copy-start(bf16[128,7296]{1,0:T(8,128)(2,1)S(1)} %fusion.157) | copy-start | bytes 5603332
  453.5 347.0 %all-gather.12.cloned.1.call-start = ((), (), s32[]{:S(2)}) async-start(), calls=%async_computation.3 | async-start | bytes 10584064 | tf_op jit(solution)/shard_map/all_gather | solution.py:61
  545.9 8.9 collective-permute-start.4
  583.7 12.1 %copy-start.2 = (bf16[128,2432]{1,0:T(8,128)(2,1)S(1)}, bf16[128,2432]{1,0:T(8,128)(2,1)}, u32[]{:S(2)}) copy-start(bf16[128,2432]{1,0:T(8,128)(2,1)} %copy.62) | copy-start | bytes 1867780
  649.1 42.2 %collective-permute-start.5 = (bf16[3,64,2432]{2,1,0:T(8,128)(2,1)S(1)}, bf16[3,64,2432]{2,1,0:T(8,128)(2,1)S(1)}, u32[]{:S(2)}, u32[]{:S(2)}) collective-permute-start(bf16[3,64,2432]{2,1,0:T(8,128)(2,1)S(1)} %slice.162), channel_id=1, source_target_pairs={{0,2},{1,3},{2,0},{3,1},{4,6},{5,7},{6,4},{7,5},{8,10},{9,11},{10,... | collective-permute-start | bytes 2801672 | tf_op jit(solution)/shard_map/ppermute | solution.py:78
  717.4 266.8 %all-gather.14.cloned.1.call-start = ((), (), s32[]{:S(2)}) async-start(), calls=%async_computation.4 | async-start | bytes 10584064 | tf_op jit(solution)/shard_map/all_gather | solution.py:61
Sparse Core Ops, SparseCore 0:
  38.7 101.6 all-gather.5
  251.0 91.9 all-gather.7
  453.6 92.2 all-gather.9
  717.6 82.9 all-gather.11
  901.9 82.3 all-gather.13
where the time goes:
time: 1080 us; the launch traced here: 1070 us
  waiting for transfers between devices  487 us (45%)
  matrix products  371 us (34%)
  local copies, waits for them, and re-layouts  160 us (15%)
  starting transfers between devices  26.6 us (2%)
  other arithmetic  15.9 us (1%)
  between operations  13.8 us (1%)
    all_gather x3, waiting for transfers between devices, gather_branch(): gathered = lax.all_gather(kv_rows, 'seq', axis=0, tiled=True)  286 us
    dot_general x13, matrix products, project(): jnp.einsum('...d,de->...e', act_rows, weight, preferred_element_type=jnp....  261 us
    all_gather x2, waiting for transfers between devices, gather_image(): return lax.all_gather(kv_rows, ('seq', 'branch'), axis=0, tiled=True)  164 us
    slice x10, local copies, waits for them, and re-layouts, run_block(): k_heads = kv_all[:, :model_width].reshape(key_count, num_heads, head_dim)  79.6 us
    dot_general x5, matrix products, run_block(): jnp.einsum('qhc,hcd->qd', mixed_rows, w_proj, preferred_element_type=jnp....  66.1 us
    slice x5, local copies, waits for them, and re-layouts, run_block(): v_heads = kv_all[:, model_width:].reshape(key_count, num_heads, head_dim)  38.2 us
    sub x3, matrix products, run_block(): attn_probs = jax.nn.softmax(scores, axis=-1).astype(jnp.bfloat16)  35.9 us
  transfers between devices with their start and end apart: 11, of which 10 were waited for; matrix products, arithmetic and copies ran while one was open for 2% of the time, Pallas kernels for 0%

commit v1 on v0

v1 whole, which is shorter than its diff:
```python
import functools
import jax
import jax.numpy as jnp
from jax import lax
from jax.experimental import pallas as pl
from jax.experimental.pallas import tpu as pltpu
from jax.sharding import PartitionSpec as P

EPS = 1e-6
D = 2432
HALF_UP = 4864
LANES = 128
TOK = 1024
SLOTS = 60
MESH_ID = pl.DeviceIdType.MESH
BF16 = jnp.bfloat16
F32 = jnp.float32


def aligned(value, unit):
    return value if isinstance(value, int) else pl.multiple_of(value, unit)


class WeightRing:
    def __init__(self, segments, buf, sem):
        self.buf, self.sem = buf, sem
        self.bounds = []
        first = 0
        for count, source in segments:
            self.bounds.append((first, first + count, source))
            first += count
        self.total = first
        self.any_source = segments[0][1](0)

    def start(self, base, off, span):
        unit = base + off
        for first, last, source in self.bounds:
            lo, hi = max(first, base), min(last, base + span)
            if lo >= hi or isinstance(unit, int) and not first <= unit < last:
                continue

            def issue(first=first, source=source):
                slot = lax.rem(jnp.int32(unit), SLOTS)
                pltpu.make_async_copy(source(unit - first), self.buf.at[slot], self.sem.at[slot]).start()

            if isinstance(unit, int) or lo == base and hi == base + span:
                issue()
            else:
                pl.when(jnp.logical_and(unit >= first, unit < last))(issue)

    def fill(self):
        for first, last, source in self.bounds:
            last = min(last, SLOTS)
            if first >= last:
                break

            @pl.loop(first, last)
            def _(unit, first=first, source=source):
                pltpu.make_async_copy(source(unit - first), self.buf.at[unit], self.sem.at[unit]).start()

    def wait(self, unit):
        slot = lax.rem(jnp.int32(unit), SLOTS)
        pltpu.make_async_copy(self.any_source, self.buf.at[slot], self.sem.at[slot]).wait()
        return slot

    def load(self, units):
        slots = [self.wait(unit) for unit in units]
        parts = [self.buf[slot] for slot in slots]
        return parts[0] if len(parts) == 1 else jnp.concatenate(parts, axis=1)


def matmul(lhs, rhs):
    return jnp.dot(lhs, rhs, preferred_element_type=F32)


def add_f32(left, right):
    return left.astype(F32) + right.astype(F32)


def ln_rows(src, dst, rows):
    for r0 in range(0, rows, 32):
        val = src[r0:r0 + 32, :].astype(F32)
        cen = val - jnp.mean(val, axis=-1, keepdims=True)
        var = jnp.mean(cen * cen, axis=-1, keepdims=True)
        dst[r0:r0 + 32, :] = (cen * lax.rsqrt(var + EPS)).astype(BF16)


def step_kernel(num_in, lat, hint, in_qkv, in_proj, in_up, in_down, out_qkv, out_proj, out_up, out_down, hint_w, zero_w, skip_w, final_w, y_ref,
                wbuf, xl, hi, msg, u, x, act, po, ps, pin, qin, stg, o_st, a_in, vv, part, rx, skp,
                wsem, init_sem, xs_sem, xr_sem, us_sem, ur_sem, qs_sem, qr_sem, as_sem, ar_sem, ps_sem, pr_sem, es_sem, er_sem):
    data_id = lax.axis_index('data')
    seq_id = lax.axis_index('seq')
    branch_id = lax.axis_index('branch')
    core = branch_id % 2
    row_y = branch_id // 2
    side = seq_id // 2
    quad = 2 * row_y + seq_id % 2
    chip = 4 * side + quad

    def device(side_id, quad_id, core_id):
        return (data_id, 2 * side_id + quad_id % 2, 2 * (quad_id // 2) + core_id)

    peer = device(side, quad, 1 - core)
    partner = device(1 - side, quad, core)

    def remote(src, dst, send, recv, dev):
        return pltpu.make_async_remote_copy(src_ref=src, dst_ref=dst, send_sem=send, recv_sem=recv, device_id=dev, device_id_type=MESH_ID)

    def layout(is_in):
        n_chips = 4 if is_in else 8
        me = quad if is_in else chip
        bits = 2 if is_in else 3

        def extra_dest(idx):
            return 2 * idx + core if is_in else 1 + 5 * idx + 3 * core

        def combo(j):
            extra = j // 8
            rel = (n_chips - 1) - j % n_chips
            prim = 0
            for bit in range(bits):
                step = 2 ** bit
                prim = prim + step * ((me // step + rel // step) % 2)
            slot_p = j // n_chips
            num_p = 10 * core + slot_p * n_chips + prim
            num_x = 10 * core + j
            num_x = num_x - num_x // 19
            dest = (1 - extra) * prim + extra * extra_dest(j - 8)
            slot = (1 - extra) * slot_p + extra * (8 // n_chips)
            num = (1 - extra) * num_p + extra * num_x
            return dest, slot, num, j + core < 10

        def owner(num):
            plane, j = num // 10, num % 10
            if j < 8:
                return plane, j % n_chips
            return plane, (2 * (j - 8) + plane if is_in else 1 + 5 * (j - 8) + 3 * plane)

        return n_chips, me, combo, owner, extra_dest

    def chip_device(is_in, idx, core_id):
        return device(side, idx, core_id) if is_in else device(idx // 4, idx % 4, core_id)

    def cols(start):
        return pl.ds(aligned(start, LANES), LANES)

    def square(ref, *lead):
        return (19, lambda j: ref.at[(*lead, slice(None), cols(j * LANES))])

    def qkv_segment(is_in, *lead):
        ref = in_qkv if is_in else out_qkv
        combo = layout(is_in)[2]
        return (30, lambda j: ref.at[(*lead, slice(None), cols((j % 3) * D + combo(j // 3)[2] * LANES))])

    def up_segment(ref, *lead):
        return (38, lambda j: ref.at[(*lead, slice(None), cols(core * HALF_UP + j * LANES))])

    def down_segment(ref, *lead):
        def source(j):
            last, tile, r = j // 36, j // 4, j % 4
            k_sub = (1 - last) * (r // 2) + last * r
            col = 2 * tile + (1 - last) * (r % 2)
            return ref.at[(*lead, pl.ds(aligned(core * HALF_UP + k_sub * D, LANES), D), cols(col * LANES))]
        return (38, source)

    def skip_segment(idx, half):
        return (19, lambda j: skip_w.at[idx, pl.ds(half * D, D), cols(j * LANES)])

    num_out = num_in
    segments = []
    marks = {}

    def put(name, segment):
        marks[name] = sum(seg[0] for seg in segments)
        segments.append(segment)

    put('hint', square(hint_w))
    for blk in range(num_in + 1):
        put(('qkv', 1, blk), qkv_segment(True, side, blk))
        if blk > 0:
            put(('zero', blk - 1), square(zero_w, blk - 1))
        put(('proj', 1, blk), square(in_proj, side, blk))
        put(('up', 1, blk), up_segment(in_up, side, blk))
        put(('down', 1, blk), down_segment(in_down, side, blk))
    put(('zero', num_in), square(zero_w, num_in))
    put(('skip_s', 0), skip_segment(0, 1))
    put(('skip_o', 0), skip_segment(0, 0))
    for blk in range(num_out):
        put(('qkv', 0, blk), qkv_segment(False, blk))
        if blk + 1 < num_out:
            put(('skip_s', blk + 1), skip_segment(blk + 1, 1))
        put(('proj', 0, blk), square(out_proj, blk))
        put(('up', 0, blk), up_segment(out_up, blk))
        put(('down', 0, blk), down_segment(out_down, blk))
        if blk + 1 < num_out:
            put(('skip_o', blk + 1), skip_segment(blk + 1, 0))
    put('final', square(final_w))
    ring = WeightRing(segments, wbuf, wsem)

    def mm(name, units, lhs, emit, k_subs=1):
        first = marks[name]
        per = 2 * k_subs

        def tile(t, width):
            base = t * per
            acc = None
            for k in range(k_subs):
                rhs = ring.load([first + base + k * width + i for i in range(width)])
                term = matmul(lhs(k), rhs)
                acc = term if acc is None else acc + term
            emit(aligned(t * 256, 256), width * LANES, acc)
            for r in range(width * k_subs):
                ring.start(first + SLOTS, base + r, units)

        pl.loop(0, units // per)(lambda t: tile(t, 2))
        if units % per:
            tile(units // per, 1)

    get_lat = pltpu.make_async_copy(lat.at[0], xl, init_sem.at[0])
    get_hint = pltpu.make_async_copy(hint.at[0], hi, init_sem.at[1])
    get_hint.start()
    get_lat.start()
    ring.fill()
    barrier = pltpu.get_barrier_semaphore()
    my_index = seq_id * 4 + branch_id
    for k in range(1, 16):
        other = (my_index + k) % 16
        pl.semaphore_signal(barrier, inc=1, device_id=(data_id, other // 4, other % 4), device_id_type=MESH_ID)
    pl.semaphore_wait(barrier, 15)
    get_lat.wait()
    get_hint.wait()

    mine = pl.ds(pl.multiple_of(side * 64, 64), 64)
    theirs = pl.ds(pl.multiple_of((1 - side) * 64, 64), 64)

    def emit_hint(col, width, acc):
        base_in = xl[:, pl.ds(col, width)]
        control_in = add_f32(base_in, acc.astype(BF16)).astype(BF16)
        is_base = side == 0
        u[mine, pl.ds(col, width)] = jnp.where(is_base, base_in, control_in)
        msg[:, pl.ds(col, width)] = jnp.where(is_base, control_in, base_in)

    mm('hint', 19, lambda k: hi[...], emit_hint)
    swap = remote(msg, u.at[mine], us_sem, ur_sem, partner)
    swap.start()
    swap.wait()

    def exchange_rows(rows):
        ln_rows(u, x, rows)
        send = remote(x.at[pl.ds(0, rows)], x.at[pl.ds(rows, rows)], xs_sem, xr_sem, peer)
        send.start()
        send.wait_recv()
        return send

    def run_block(is_in, blk, fill_in, before_proj):
        rows = 128 if is_in else 64
        chip_rows = 2 * rows
        n_chips, me, combo, owner, extra_dest = layout(is_in)
        key = (1 if is_in else 0, blk)
        extra_slot = 8 // n_chips

        sent = exchange_rows(rows)

        def piece_copy(j, dest, slot):
            return remote(stg.at[j, pl.ds(0, chip_rows)], qin.at[slot, pl.ds(pl.multiple_of(me * chip_rows, chip_rows), chip_rows)],
                          qs_sem.at[j], qr_sem.at[slot, me], chip_device(is_in, dest, core))

        first = marks[('qkv',) + key]

        @pl.loop(0, 10)
        def _(j):
            dest, slot, num, valid = combo(j)
            rhs = ring.load([first + 3 * j + i for i in range(3)])

            @pl.when(valid)
            def _():
                stg[j, 0:chip_rows, :] = matmul(x[0:chip_rows, :], rhs).astype(BF16)

                @pl.when(dest != me)
                def _():
                    piece_copy(j, dest, slot).start()

                @pl.when(dest == me)
                def _():
                    qin[slot, pl.ds(pl.multiple_of(me * chip_rows, chip_rows), chip_rows), :] = stg[j, 0:chip_rows, :]

            for i in range(3):
                ring.start(first + SLOTS, 3 * j + i, 30)

        sent.wait_send()
        fill_in()

        def send_copies(slot, num):
            copies = []
            col = cols(num * LANES)
            for k in range(n_chips):
                idx = (me + k) % n_chips
                for which in range(2):
                    if k == 0 and which == 0:
                        continue
                    to_core = core if which == 0 else 1 - core
                    src = o_st.at[slot, pl.ds(pl.multiple_of(idx * chip_rows + which * rows, rows), rows)]
                    copies.append(remote(src, a_in.at[pl.ds(0, rows), col], as_sem.at[slot, 2 * k + which], ar_sem.at[num], chip_device(is_in, idx, to_core)))
            return copies

        def attend(slot, num):
            for k in range(1, n_chips):
                src = (me + k) % n_chips
                remote(stg.at[0, pl.ds(0, chip_rows)], qin.at[slot, pl.ds(pl.multiple_of(src * chip_rows, chip_rows), chip_rows)],
                       qs_sem.at[0], qr_sem.at[slot, src], peer).wait_recv()
            low = lax.broadcasted_iota(jnp.int32, (TOK, LANES), 1) < 64
            v_pair = qin[slot, :, 2 * LANES:3 * LANES]
            zero = jnp.zeros_like(v_pair)
            vv[0:TOK, :] = jnp.where(low, v_pair, zero)
            vv[TOK:2 * TOK, :] = jnp.where(low, zero, v_pair)

            @pl.loop(0, TOK // 128)
            def _(i):
                q_rows = pl.ds(pl.multiple_of(i * 128, 128), 128)
                q_pair = (qin[slot, q_rows, 0:LANES].astype(F32) * 0.125).astype(BF16)
                low_q = lax.broadcasted_iota(jnp.int32, (128, LANES), 1) < 64
                none = jnp.zeros_like(q_pair)
                q_both = jnp.concatenate([jnp.where(low_q, q_pair, none), jnp.where(low_q, none, q_pair)], axis=0)
                scores = lax.dot_general(q_both, qin[slot, :, LANES:2 * LANES], (((1,), (1,)), ((), ())), preferred_element_type=F32)
                weights = jnp.exp(scores - jnp.max(scores, axis=-1, keepdims=True))
                inv = 1.0 / jnp.sum(weights, axis=-1, keepdims=True)
                probs = weights.astype(BF16)
                mixed = matmul(jnp.concatenate([probs[0:128], probs[128:256]], axis=1), vv[...])
                o_st[slot, q_rows, :] = (mixed * jnp.where(low_q, inv[0:128], inv[128:256])).astype(BF16)

            a_in[0:rows, cols(num * LANES)] = o_st[slot, pl.ds(pl.multiple_of(me * chip_rows, chip_rows), rows), :]
            for copy in send_copies(slot, num):
                copy.start()

        for slot in range(extra_slot):
            attend(slot, 10 * core + slot * n_chips + me)
        holds_first = extra_dest(0) == me
        holds_second = jnp.logical_and(extra_dest(1) == me, core == 0)
        extra_num = 10 * core + 8 + holds_second.astype(jnp.int32)
        holds_extra = jnp.logical_or(holds_first, holds_second)

        @pl.when(holds_extra)
        def _():
            attend(extra_slot, extra_num)

        @pl.loop(0, 10)
        def _(j):
            dest, slot, num, valid = combo(j)

            @pl.when(jnp.logical_and(valid, dest != me))
            def _():
                piece_copy(j, dest, slot).wait_send()

        for num in range(19):
            plane, dest = owner(num)

            @pl.when(jnp.logical_not(jnp.logical_and(core == plane, me == dest)))
            def _(num=num):
                remote(o_st.at[0, pl.ds(0, rows)], a_in.at[pl.ds(0, rows), num * LANES:(num + 1) * LANES], as_sem.at[0, 0], ar_sem.at[num], peer).wait_recv()

        before_proj()

        def emit_proj(col, width, acc):
            u[0:rows, pl.ds(col, width)] = add_f32(u[0:rows, pl.ds(col, width)], acc.astype(BF16)).astype(BF16)

        mm(('proj',) + key, 19, lambda k: a_in[0:rows, :], emit_proj)

        for slot in range(extra_slot):
            for copy in send_copies(slot, 10 * core + slot * n_chips + me):
                copy.wait_send()

        @pl.when(holds_extra)
        def _():
            for copy in send_copies(extra_slot, extra_num):
                copy.wait_send()

        sent = exchange_rows(rows)

        def emit_up(col, width, acc):
            hidden = acc.astype(BF16).astype(F32)
            act[0:chip_rows, pl.ds(col, width)] = jax.nn.gelu(hidden).astype(BF16)

        mm(('up',) + key, 38, lambda k: x[0:chip_rows, :], emit_up)

        def partial_copy(col, width):
            tile = col // 256
            return remote(ps.at[pl.ds(0, rows), pl.ds(col, width)], pin.at[pl.ds(0, rows), pl.ds(col, width)], ps_sem.at[tile], pr_sem.at[tile], peer)

        def emit_down(col, width, acc):
            po[0:rows, pl.ds(col, width)] = acc[0:rows]
            ps[0:rows, pl.ds(col, width)] = acc[rows:chip_rows]
            partial_copy(col, width).start()

        sent.wait_send()
        mm(('down',) + key, 38, lambda k: act[0:chip_rows, k * D:(k + 1) * D], emit_down, k_subs=2)

        def finish(col, width):
            partial_copy(col, width).wait()
            total = (po[0:rows, pl.ds(col, width)] + pin[0:rows, pl.ds(col, width)]).astype(BF16)
            u[0:rows, pl.ds(col, width)] = add_f32(u[0:rows, pl.ds(col, width)], total).astype(BF16)

        pl.loop(0, 9)(lambda t: finish(aligned(t * 256, 256), 256))
        finish(9 * 256, LANES)

    def make_part(idx):
        def emit(col, width, acc):
            part[idx, :, pl.ds(col, width)] = jnp.where(side == 0, u[:, pl.ds(col, width)], acc.astype(BF16))
        mm(('zero', idx), 19, lambda k: u[...], emit)

    def part_copy(idx):
        return remote(part.at[idx, theirs], rx.at[idx], es_sem.at[idx], er_sem.at[idx], partner)

    nothing = lambda: None
    for blk in range(num_in + 1):
        if blk == 0:
            run_block(True, blk, nothing, nothing)
        else:
            run_block(True, blk, functools.partial(make_part, blk - 1), lambda blk=blk: part_copy(blk - 1).start())
    make_part(num_in)
    part_copy(num_in).start()
    for idx in range(num_in):
        part_copy(idx).wait()
        rx[idx] = add_f32(part[idx, mine, :], rx[idx]).astype(BF16)

    def skip_part(blk):
        def emit(col, width, acc):
            skp[:, pl.ds(col, width)] = acc
        mm(('skip_s', blk), 19, lambda k: rx[num_in - 1 - blk], emit)

    def merge(blk):
        def emit(col, width, acc):
            msg[:, pl.ds(col, width)] = (skp[:, pl.ds(col, width)] + acc).astype(BF16)
        mm(('skip_o', blk), 19, lambda k: u[0:64, :], emit)
        u[0:64, :] = msg[...]

    skip_part(0)
    part_copy(num_in).wait()
    u[0:64, :] = add_f32(part[num_in, mine, :], rx[num_in]).astype(BF16)
    for blk in range(num_out):
        merge(blk)
        run_block(False, blk, functools.partial(skip_part, blk + 1) if blk + 1 < num_out else nothing, nothing)

    ln_rows(u, x, 64)

    def emit_final(col, width, acc):
        y_ref[0, :, pl.ds(col, width)] = acc.astype(BF16)

    mm('final', 19, lambda k: x[0:64, :], emit_final)


def solution(mesh):
    row_spec = P('data', ('seq', 'branch'), None)

    def device_fn(latents, hint_emb, in_qkv, in_proj, in_up, in_down, out_qkv, out_proj, out_up, out_down, hint_proj, zero_proj, skip_proj, final_proj):
        num_in = out_qkv.shape[0]
        in_proj = in_proj.reshape(2, num_in + 1, D, D)
        out_proj = out_proj.reshape(num_in, D, D)
        anywhere = pl.BlockSpec(memory_space=pl.ANY)
        dma = pltpu.SemaphoreType.DMA
        return pl.pallas_call(
            functools.partial(step_kernel, num_in),
            out_shape=jax.ShapeDtypeStruct((1, 64, D), BF16),
            in_specs=[anywhere] * 14,
            out_specs=pl.BlockSpec(memory_space=pltpu.VMEM),
            scratch_shapes=[
                pltpu.VMEM((SLOTS, D, LANES), BF16),
                pltpu.VMEM((64, D), BF16),
                pltpu.VMEM((64, D), BF16),
                pltpu.VMEM((64, D), BF16),
                pltpu.VMEM((128, D), BF16),
                pltpu.VMEM((256, D), BF16),
                pltpu.VMEM((256, HALF_UP), BF16),
                pltpu.VMEM((128, D), F32),
                pltpu.VMEM((128, D), F32),
                pltpu.VMEM((128, D), F32),
                pltpu.VMEM((3, TOK, 3 * LANES), BF16),
                pltpu.VMEM((10, 256, 3 * LANES), BF16),
                pltpu.VMEM((3, TOK, LANES), BF16),
                pltpu.VMEM((128, D), BF16),
                pltpu.VMEM((2 * TOK, LANES), BF16),
                pltpu.VMEM((num_in + 1, 128, D), BF16),
                pltpu.VMEM((num_in + 1, 64, D), BF16),
                pltpu.VMEM((64, D), F32),
                dma((SLOTS,)), dma((2,)), dma, dma, dma, dma,
                dma((10,)), dma((3, 8)), dma((3, 16)), dma((19,)),
                dma((10,)), dma((10,)), dma((num_in + 1,)), dma((num_in + 1,)),
            ],
            compiler_params=pltpu.CompilerParams(collective_id=0, has_side_effects=True, vmem_limit_bytes=67043328),
            name='denoiser_step',
        )(latents, hint_emb, in_qkv, in_proj, in_up, in_down, out_qkv, out_proj, out_up, out_down, hint_proj, zero_proj, skip_proj, final_proj)

    return jax.shard_map(device_fn, mesh=mesh, in_specs=(row_spec, row_spec) + (P(),) * 12, out_specs=row_spec, check_vma=False)
```

time: 1080 us -> 374 us (0.35)
  waiting for transfers between devices: 487 us -> 0 us
  Pallas kernels: 0 us -> 372 us
  matrix products: 371 us -> 0 us
  local copies, waits for them, and re-layouts: 160 us -> 1.71 us
  starting transfers between devices: 26.6 us -> 0 us
  other arithmetic: 15.9 us -> 0 us
  between operations: 13.8 us -> 0.01 us
    all_gather x5 -> x0, waiting for transfers between devices: 450 us -> none  [the longest x3 286 us: gather_branch(): gathered = lax.all_gather(kv_rows, 'seq', axis=0, tiled=True)]
    pallas_call x0 -> x1, Pallas kernels: none -> 372 us  [device_fn(): pl.pallas_call(functools.partial(step_kernel, num_in), out_shape=jax.Shap...]
    dot_general x20 -> x0, matrix products: 335 us -> none  [the longest x13 261 us: project(): jnp.einsum('...d,de->...e', act_rows, weight, preferred_element_type=jnp....]
    slice x29 -> x0, local copies, waits for them, and re-layouts: 127 us -> none  [the longest x10 79.6 us: run_block(): k_heads = kv_all[:, :model_width].reshape(key_count, num_heads, head_dim)]
    ppermute x6 -> x0, waiting for transfers between devices: 36.4 us -> none  [the longest x1 21.4 us: device_fn(): received = lax.ppermute(part_stack[:, own_count:], 'branch', swap_perm)]
    sub x3 -> x0, matrix products: 35.9 us -> none  [run_block(): attn_probs = jax.nn.softmax(scores, axis=-1).astype(jnp.bfloat16)]
    ppermute x6 -> x0, starting transfers between devices: 25.7 us -> none  [the longest x1 20.8 us: device_fn(): received = lax.ppermute(part_stack[:, own_count:], 'branch', swap_perm)]
    unnamed x14 -> x1, local copies, waits for them, and re-layouts: 16.7 us -> 1.71 us
  transfers between devices with their start and end apart: 11 -> 0, of which waited for: 10 -> 0; matrix products, arithmetic and copies ran while one was open for 2% -> 0% of each run, Pallas kernels for 0% -> 0%
where the time goes in v1:
time: 374 us
  Pallas kernels  372 us (99%)
    pallas_call x1, Pallas kernels, device_fn(): pl.pallas_call(functools.partial(step_kernel, num_in), out_shape=jax.Shap...  372 us

profile of v1, /device:TPU:0, one launch (start us, length us, event | category | flops | bytes accessed | tf_op | source)
XLA Modules:
  0.0 374.2 jit_solution(16064504640785298371)
XLA Ops:
  0.0 372.5 %denoiser_step.1 = bf16[1,64,2432]{2,1,0:T(8,128)(2,1)} custom-call(bf16[1,64,2432]{2,1,0:T(8,128)(2,1)} %lat.1, bf16[1,64,2432]{2,1,0:T(8,128)(2,1)} %hint.1, bf16[2,3,2432,7296]{3,2,1,0:T(8,128)(2,1)} %in_qkv.1, bf16[2,3,2432,2432]{3,2,1,0:T(8,128)(2,1)} %bitcast.in_proj, bf16[2,3,2432,9728]{3,2,1,0:T(8,128)(2,1)} %in_up.1, ...), custom_call_target="tpu_custom_call" | custom-call | tf_op jit(solution)/shard_map/denoiser_step/pallas_call | solution.py:460
  372.5 1.7 copy.16
